TPU v7x, 32 devices: a whole 2x2x4 slice. The times are simulated.
32 devices in a mesh: tp: 8 (over z, core), fs: 4 (over y, x).
Axes of the slice: x: 2, y: 2, z: 4, core: 2. Of those that a mesh axis runs over, the one named last changes fastest.
Arguments:
- tokens: bfloat16 [128, 8192], P(('tp', 'fs')), may hold values from -6 to 6
- gate_weight: bfloat16 [8192, 29568], P('fs', 'tp'), may hold values from -0.0625 to 0.0625
- up_weight: bfloat16 [8192, 29568], P('fs', 'tp'), may hold values from -0.0625 to 0.0625
- down_weight: bfloat16 [29568, 8192], P('tp', 'fs'), may hold values from -0.046875 to 0.046875
Outputs:
- mixed: bfloat16 [128, 8192], P(None, ('fs', 'tp'))
All inputs are finite; a program needn't handle non-finite values.
Results may differ from a plain program's by a relative error of at most 0.0049.
Values may be sent and summed in bfloat16 or wider, within the bound.
A program may use at most 128 MiB of HBM per device.

v0:
```python
import jax
import jax.numpy as jnp
from jax import lax
from jax.sharding import PartitionSpec as P


def body(tokens, gate_weight, up_weight, down_weight):
    by_feature = lax.all_to_all(tokens, "fs", split_axis=1, concat_axis=0, tiled=True)
    feature_rows = lax.all_gather(by_feature, "tp", axis=0, tiled=True)
    gate_part = jnp.dot(feature_rows, gate_weight, preferred_element_type=jnp.float32)
    up_part = jnp.dot(feature_rows, up_weight, preferred_element_type=jnp.float32)
    gate, up = (
        lax.psum_scatter(gate_part, "fs", scatter_dimension=1, tiled=True),
        lax.psum_scatter(up_part, "fs", scatter_dimension=1, tiled=True),
    )
    hidden = (jax.nn.silu(gate) * up).astype(jnp.bfloat16)
    hidden_all = lax.all_gather(hidden, "fs", axis=1, tiled=True)
    partial_out = jnp.dot(hidden_all, down_weight, preferred_element_type=jnp.float32)
    summed = lax.psum_scatter(partial_out, "tp", scatter_dimension=1, tiled=True)
    return summed.astype(jnp.bfloat16)


def solution(mesh):
    return jax.shard_map(
        body,
        mesh=mesh,
        in_specs=(P(("tp", "fs"), None), P("fs", "tp"), P("fs", "tp"), P("tp", "fs")),
        out_specs=P(None, ("fs", "tp")),
        check_vma=False,
    )
```

profile of v0, /device:TPU:0, one launch (start us, length us, event | category | flops | bytes accessed | tf_op | source)
XLA Modules:
  0.0 184.2 jit_solution(5929641926974322343)
XLA Ops:
  6.5 0.0 reduce-scatter.6.cloned.1.call-start
  6.5 10.0 %all_to_all.19 = bf16[4,4,2048]{2,0,1:T(4,128)(2,1)S(1)} all-to-all(bf16[4,4,2048]{2,0,1:T(4,128)(2,1)} %bitcast.19), channel_id=1, replica_groups=mesh['tp'=8,'fs'=4] {'fs'}, dimensions={1} | all-to-all | bytes 131072 | tf_op jit(solution)/shard_map/all_to_all | solution.py:8
  16.6 0.0 copy-start
  16.6 15.1 %all_gather.6 = bf16[128,2048]{1,0:T(8,128)(2,1)S(1)} all-gather(bf16[16,2048]{1,0:T(8,128)(2,1)S(1)} %all_to_all.17), channel_id=1, replica_groups=mesh['tp'=8,'fs'=4] {'tp'}, dimensions={0}, use_global_device_ids=true | all-gather | bytes 589824 | tf_op jit(solution)/shard_map/all_gather | solution.py:9
  31.8 7.6 %fusion.5 = f32[128,3696]{0,1:T(8,128)S(1)} fusion(bf16[128,2048]{1,0:T(8,128)(2,1)S(1)} %all_gather.6, bf16[2048,3696]{0,1:T(8,128)(2,1)} %param.5), kind=kOutput, calls=%fused_computation.3 | convolution fusion | flops 1937768448 | bytes 17555456 | tf_op jit(solution)/shard_map/dot_general | solution.py:10
  39.3 0.0 copy-done
  39.3 0.0 copy-start.1
  39.4 5.6 %fusion.6 = f32[128,3696]{0,1:T(8,128)} fusion(bf16[128,2048]{1,0:T(8,128)(2,1)S(1)} %all_gather.6, bf16[2048,3696]{0,1:T(8,128)(2,1)S(1)} %copy-done), kind=kOutput, calls=%fused_computation.4 | convolution fusion | flops 1937768448 | bytes 17555456 | tf_op jit(solution)/shard_map/dot_general | solution.py:11
  44.9 67.6 %fusion.4 = (f32[128,928]{0,1:T(8,128)S(1)}, f32[128,928]{0,1:T(8,128)S(1)}) fusion(f32[128,3696]{0,1:T(8,128)} %fusion.6, f32[128,3696]{0,1:T(8,128)S(1)} %fusion.5), kind=kCustom, calls=%all-reduce-scatter.2 | all-reduce-scatter fusion | flops 950273 | bytes 4735488
  112.6 1.7 collective-permute-start
  114.3 4.3 %collective-permute-start.1 = (f32[128,12]{0,1:T(8,128)S(1)}, f32[128,12]{0,1:T(8,128)S(1)}, u32[]{:S(2)}, u32[]{:S(2)}) collective-permute-start(f32[128,12]{0,1:T(8,128)S(1)} %slice.1), channel_id=1, source_target_pairs={{0,1},{1,2},{2,3},{4,5},{5,6},{6,7},{8,9},{9,10},{10,11},{12,13},{... | collective-permute-start | bytes 18440
  118.6 0.0 copy-done.1
  118.6 0.6 dynamic-slice.6
  119.9 0.0 collective-permute-done
  119.9 1.1 concatenate
  121.0 0.0 collective-permute-done.1
  121.0 1.1 concatenate.1
  122.1 0.2 fusion.3
  122.3 12.0 %all-gather = bf16[4,924,128]{2,1,0:T(8,128)(2,1)S(1)} all-gather(bf16[1,924,128]{2,1,0:T(8,128)(2,1)S(1)} %fusion.3), channel_id=1, replica_groups=mesh['tp'=8,'fs'=4] {'fs'}, dimensions={0}, use_global_device_ids=true | all-gather | bytes 1182720 | tf_op jit(solution)/shard_map/all_gather | solution.py:17
  134.3 0.2 reshape.4
  134.5 8.5 %fusion.7 = f32[128,2048]{1,0:T(8,128)} fusion(bf16[3696,128]{1,0:T(8,128)(2,1)S(1)} %reshape.4, bf16[3696,2048]{1,0:T(8,128)(2,1)} %param.7), kind=kOutput, calls=%fused_computation.5 | convolution fusion | flops 1937768448 | bytes 17133568 | tf_op jit(solution)/shard_map/dot_general | solution.py:18
  143.0 0.0 reduce-scatter.6.cloned.1.call-update
  143.0 32.8 %reduce-scatter.6.cloned.1.call-done = f32[128,256]{1,0:T(8,128)} async-done(((f32[128,2048]{1,0:T(8,128)}), f32[128,256]{1,0:T(8,128)}) %reduce-scatter.6.cloned.1.call-update) | async-done | bytes 131088 | tf_op jit(solution)/shard_map/reduce_scatter | solution.py:19
  175.8 1.5 convert_element_type.7
  (3 shorter events, 0.0 us)
Async XLA Ops:
  6.5 169.3 %reduce-scatter.6.cloned.1.call-start = ((), (), s32[]{:S(2)}) async-start(), calls=%async_computation.2 | async-start | bytes 1179648 | tf_op jit(solution)/shard_map/reduce_scatter | solution.py:19
  16.6 22.7 %copy-start = (bf16[2048,3696]{0,1:T(8,128)(2,1)S(1)}, bf16[2048,3696]{0,1:T(8,128)(2,1)}, u32[]{:S(2)}) copy-start(bf16[2048,3696]{0,1:T(8,128)(2,1)} %param.6) | copy-start | bytes 45416452
  39.3 79.3 %copy-start.1 = (u32[32]{0:T(128)S(1)}, u32[32]{0:T(128)}, u32[]{:S(2)}) copy-start(u32[32]{0:T(128)} %constant.6) | copy-start | bytes 388
  112.6 7.3 %collective-permute-start = (f32[128,12]{0,1:T(8,128)S(1)}, f32[128,12]{0,1:T(8,128)S(1)}, u32[]{:S(2)}, u32[]{:S(2)}) collective-permute-start(f32[128,12]{0,1:T(8,128)S(1)} %slice), channel_id=1, source_target_pairs={{0,1},{1,2},{2,3},{4,5},{5,6},{6,7},{8,9},{9,10},{10,11},{12,13},{... | collective-permute-start | bytes 18440
  114.3 6.7 %collective-permute-start.1 = (f32[128,12]{0,1:T(8,128)S(1)}, f32[128,12]{0,1:T(8,128)S(1)}, u32[]{:S(2)}, u32[]{:S(2)}) collective-permute-start(f32[128,12]{0,1:T(8,128)S(1)} %slice.1), channel_id=1, source_target_pairs={{0,1},{1,2},{2,3},{4,5},{5,6},{6,7},{8,9},{9,10},{10,11},{12,13},{... | collective-permute-start | bytes 18440
Sparse Core Ops, SparseCore 0:
  143.1 32.6 reduce-scatter.5
where the time goes:
time: 185 us; the launch traced here: 184 us
  blocking collectives  105 us (57%)
  waiting for transfers between devices  32.9 us (18%)
  matrix products  21.6 us (12%)
  between operations  14.2 us (8%)
  starting transfers between devices  6.01 us (3%)
  local copies, waits for them, and re-layouts  3.02 us (2%)
    unnamed x1, blocking collectives  67.6 us
    reduce_scatter x1, waiting for transfers between devices, body(): lax.psum_scatter(partial_out, 'tp', scatter_dimension=1, tiled=True)  32.8 us
    all_gather x1, blocking collectives, body(): feature_rows = lax.all_gather(by_feature, 'tp', axis=0, tiled=True)  15.1 us
    all_gather x1, blocking collectives, body(): hidden_all = lax.all_gather(hidden, 'fs', axis=1, tiled=True)  12 us
    all_to_all x1, blocking collectives, body(): lax.all_to_all(tokens, 'fs', split_axis=1, concat_axis=0, tiled=True)  10 us
    dot_general x1, matrix products, body(): jnp.dot(hidden_all, down_weight, preferred_element_type=jnp.float32)  8.5 us
    dot_general x1, matrix products, body(): jnp.dot(feature_rows, gate_weight, preferred_element_type=jnp.float32)  7.58 us
    unnamed x2, starting transfers between devices  6.01 us
  transfers between devices with their start and end apart: 3, of which 1 were waited for; matrix products, arithmetic and copies ran while one was open for 1% of the time, Pallas kernels for 0%

commit v1 on v0

--- a/solution.py
+++ b/solution.py
@@ -14,7 +14,7 @@
         lax.psum_scatter(up_part, "fs", scatter_dimension=1, tiled=True),
     )
     hidden = (jax.nn.silu(gate) * up).astype(jnp.bfloat16)
-    hidden_all = lax.all_gather(hidden, "fs", axis=1, tiled=True)
+    hidden_all = jnp.concatenate(lax.all_gather(hidden, "fs"), axis=1)
     partial_out = jnp.dot(hidden_all, down_weight, preferred_element_type=jnp.float32)
     summed = lax.psum_scatter(partial_out, "tp", scatter_dimension=1, tiled=True)
     return summed.astype(jnp.bfloat16)

time: 185 us -> 185 us (level)
  no operation moved by 1% of the time
where the time goes in v1:
time: 185 us
  blocking collectives  105 us (57%)
  waiting for transfers between devices  33.2 us (18%)
  matrix products  21.6 us (12%)
  between operations  14.2 us (8%)
  starting transfers between devices  6.01 us (3%)
  local copies, waits for them, and re-layouts  3.47 us (2%)
    unnamed x1, blocking collectives  67.6 us
    reduce_scatter x1, waiting for transfers between devices, body(): lax.psum_scatter(partial_out, 'tp', scatter_dimension=1, tiled=True)  33.2 us
    all_gather x1, blocking collectives, body(): feature_rows = lax.all_gather(by_feature, 'tp', axis=0, tiled=True)  15.1 us
    all_gather x1, blocking collectives, body(): hidden_all = jnp.concatenate(lax.all_gather(hidden, 'fs'), axis=1)  12 us
    all_to_all x1, blocking collectives, body(): lax.all_to_all(tokens, 'fs', split_axis=1, concat_axis=0, tiled=True)  10 us
    dot_general x1, matrix products, body(): jnp.dot(hidden_all, down_weight, preferred_element_type=jnp.float32)  8.5 us
    dot_general x1, matrix products, body(): jnp.dot(feature_rows, gate_weight, preferred_element_type=jnp.float32)  7.58 us
    unnamed x2, starting transfers between devices  6.01 us
  transfers between devices with their start and end apart: 3, of which 1 were waited for; matrix products, arithmetic and copies ran while one was open for 1% of the time, Pallas kernels for 0%

profile of v1, /device:TPU:0, one launch (start us, length us, event | category | flops | bytes accessed | tf_op | source)
XLA Modules:
  0.0 185.0 jit_solution(5485690145713021485)
XLA Ops:
  6.5 0.0 reduce-scatter.6.cloned.1.call-start
  6.5 10.0 %all_to_all.19 = bf16[4,4,2048]{2,0,1:T(4,128)(2,1)S(1)} all-to-all(bf16[4,4,2048]{2,0,1:T(4,128)(2,1)} %bitcast.23), channel_id=1, replica_groups=mesh['tp'=8,'fs'=4] {'fs'}, dimensions={1} | all-to-all | bytes 131072 | tf_op jit(solution)/shard_map/all_to_all | solution.py:8
  16.6 0.0 copy-start
  16.6 15.1 %all_gather.9 = bf16[128,2048]{1,0:T(8,128)(2,1)S(1)} all-gather(bf16[16,2048]{1,0:T(8,128)(2,1)S(1)} %all_to_all.17), channel_id=1, replica_groups=mesh['tp'=8,'fs'=4] {'tp'}, dimensions={0}, use_global_device_ids=true | all-gather | bytes 589824 | tf_op jit(solution)/shard_map/all_gather | solution.py:9
  31.8 7.6 %fusion.4 = f32[128,3696]{0,1:T(8,128)S(1)} fusion(bf16[128,2048]{1,0:T(8,128)(2,1)S(1)} %all_gather.9, bf16[2048,3696]{0,1:T(8,128)(2,1)} %param.5), kind=kOutput, calls=%fused_computation.3 | convolution fusion | flops 1937768448 | bytes 17555456 | tf_op jit(solution)/shard_map/dot_general | solution.py:10
  39.3 0.0 copy-done
  39.3 0.0 copy-start.1
  39.4 5.6 %fusion.5 = f32[128,3696]{0,1:T(8,128)} fusion(bf16[128,2048]{1,0:T(8,128)(2,1)S(1)} %all_gather.9, bf16[2048,3696]{0,1:T(8,128)(2,1)S(1)} %copy-done), kind=kOutput, calls=%fused_computation.4 | convolution fusion | flops 1937768448 | bytes 17555456 | tf_op jit(solution)/shard_map/dot_general | solution.py:11
  44.9 67.6 %fusion.3 = (f32[128,928]{0,1:T(8,128)S(1)}, f32[128,928]{0,1:T(8,128)S(1)}) fusion(f32[128,3696]{0,1:T(8,128)} %fusion.5, f32[128,3696]{0,1:T(8,128)S(1)} %fusion.4), kind=kCustom, calls=%all-reduce-scatter.2 | all-reduce-scatter fusion | flops 950273 | bytes 4735488
  112.6 1.7 collective-permute-start
  114.3 4.3 %collective-permute-start.1 = (f32[128,12]{0,1:T(8,128)S(1)}, f32[128,12]{0,1:T(8,128)S(1)}, u32[]{:S(2)}, u32[]{:S(2)}) collective-permute-start(f32[128,12]{0,1:T(8,128)S(1)} %slice.1), channel_id=1, source_target_pairs={{0,1},{1,2},{2,3},{4,5},{5,6},{6,7},{8,9},{9,10},{10,11},{12,13},{... | collective-permute-start | bytes 18440
  118.6 0.0 copy-done.1
  118.6 0.6 dynamic-slice.6
  119.9 0.0 collective-permute-done
  119.9 1.1 concatenate
  121.0 0.0 collective-permute-done.1
  121.0 1.1 concatenate.1
  122.1 0.2 fusion.2
  122.3 12.0 %all-gather = bf16[512,924]{0,1:T(8,128)(2,1)S(1)} all-gather(bf16[128,924]{0,1:T(8,128)(2,1)S(1)} %fusion.2), channel_id=2, replica_groups=mesh['tp'=8,'fs'=4] {'fs'}, dimensions={0}, use_global_device_ids=true | all-gather | bytes 1182720 | tf_op jit(solution)/shard_map/all_gather | solution.py:17
  134.3 0.3 reshape.11
  134.6 0.1 copy.10
  134.8 0.2 reshape.10
  134.9 8.5 %fusion.6 = f32[128,2048]{1,0:T(8,128)} fusion(bf16[128,3696]{0,1:T(8,128)(2,1)S(1)} %reshape.10, bf16[3696,2048]{1,0:T(8,128)(2,1)} %param.7), kind=kOutput, calls=%fused_computation.5 | convolution fusion | flops 1937768448 | bytes 17133568 | tf_op jit(solution)/shard_map/dot_general | solution.py:18
  143.4 0.0 reduce-scatter.6.cloned.1.call-update
  143.5 33.2 %reduce-scatter.6.cloned.1.call-done = f32[128,256]{1,0:T(8,128)} async-done(((f32[128,2048]{1,0:T(8,128)}), f32[128,256]{1,0:T(8,128)}) %reduce-scatter.6.cloned.1.call-update) | async-done | bytes 131088 | tf_op jit(solution)/shard_map/reduce_scatter | solution.py:19
  176.6 1.5 convert_element_type.7
  (3 shorter events, 0.0 us)
Async XLA Ops:
  6.5 170.1 %reduce-scatter.6.cloned.1.call-start = ((), (), s32[]{:S(2)}) async-start(), calls=%async_computation.2 | async-start | bytes 1179648 | tf_op jit(solution)/shard_map/reduce_scatter | solution.py:19
  16.6 22.7 %copy-start = (bf16[2048,3696]{0,1:T(8,128)(2,1)S(1)}, bf16[2048,3696]{0,1:T(8,128)(2,1)}, u32[]{:S(2)}) copy-start(bf16[2048,3696]{0,1:T(8,128)(2,1)} %param.6) | copy-start | bytes 45416452
  39.3 79.3 %copy-start.1 = (u32[32]{0:T(128)S(1)}, u32[32]{0:T(128)}, u32[]{:S(2)}) copy-start(u32[32]{0:T(128)} %constant.6) | copy-start | bytes 388
  112.6 7.3 %collective-permute-start = (f32[128,12]{0,1:T(8,128)S(1)}, f32[128,12]{0,1:T(8,128)S(1)}, u32[]{:S(2)}, u32[]{:S(2)}) collective-permute-start(f32[128,12]{0,1:T(8,128)S(1)} %slice), channel_id=1, source_target_pairs={{0,1},{1,2},{2,3},{4,5},{5,6},{6,7},{8,9},{9,10},{10,11},{12,13},{... | collective-permute-start | bytes 18440
  114.3 6.7 %collective-permute-start.1 = (f32[128,12]{0,1:T(8,128)S(1)}, f32[128,12]{0,1:T(8,128)S(1)}, u32[]{:S(2)}, u32[]{:S(2)}) collective-permute-start(f32[128,12]{0,1:T(8,128)S(1)} %slice.1), channel_id=1, source_target_pairs={{0,1},{1,2},{2,3},{4,5},{5,6},{6,7},{8,9},{9,10},{10,11},{12,13},{... | collective-permute-start | bytes 18440
Sparse Core Ops, SparseCore 0:
  143.6 33.0 reduce-scatter.5
